TPU v7x, 16 devices: a whole 2x2x2 slice. The times are simulated.
16 devices in a mesh: fsdp: 16 (over z, y, x, core).
Axes of the slice: x: 2, y: 2, z: 2, core: 2. Of those that a mesh axis runs over, the one named last changes fastest.
Arguments:
- tok_ids: int32 [16, 1536], P('fsdp')
- grad_out: bfloat16 [16, 1536, 1536], P('fsdp')
- emb_table: bfloat16 [151936, 1536], P('fsdp')
- norm_gain: bfloat16 [1536], P('fsdp')
- w_query: bfloat16 [1536, 1536], P('fsdp')
- b_query: bfloat16 [1536], P('fsdp')
- w_key: bfloat16 [1536, 256], P('fsdp')
- b_key: bfloat16 [256], P('fsdp')
- w_value: bfloat16 [1536, 256], P('fsdp')
- b_value: bfloat16 [256], P('fsdp')
- w_out: bfloat16 [1536, 1536], P('fsdp')
Outputs:
- output 1: bfloat16 [16, 1536, 1536], P('fsdp')
- output 2: bfloat16 [151936, 1536], P('fsdp')
- output 3: float32 [1536], P('fsdp')
- output 4: float32 [1536, 1536], P('fsdp')
- output 5: float32 [1536], P('fsdp')
- output 6: float32 [1536, 256], P('fsdp')
- output 7: float32 [256], P('fsdp')
- output 8: float32 [1536, 256], P('fsdp')
- output 9: float32 [256], P('fsdp')
- output 10: float32 [1536, 1536], P('fsdp')
All inputs are finite; a program needn't handle non-finite values.
Results may differ from a plain program's by a relative error of at most 0.0146869.
Values are sent between devices in bfloat16 or wider.
A program may use at most 1 GiB of HBM per device.

v0:
```python
import jax
import jax.numpy as jnp
from jax import lax
from jax.sharding import PartitionSpec as P

HEAD_DIM = 128
ROPE_THETA = 1.0e6
NORM_EPS = 1e-6
MASK_VALUE = -1e30


def rope_tables(seq_len):
    half_dim = HEAD_DIM // 2
    inv_freq = jnp.power(ROPE_THETA, -(jnp.arange(half_dim, dtype=jnp.float32) * 2.0 / HEAD_DIM))
    angles = jnp.arange(seq_len, dtype=jnp.float32)[:, None] * inv_freq[None, :]
    angles = jnp.concatenate([angles, angles], axis=-1)
    return jnp.cos(angles)[:, None, :], jnp.sin(angles)[:, None, :]


def rotate(vector, cos_t, sin_t):
    half_dim = HEAD_DIM // 2
    turned = jnp.concatenate([-vector[..., half_dim:], vector[..., :half_dim]], axis=-1)
    return vector * cos_t + turned * sin_t


def rotate_back(grad_in, cos_t, sin_t):
    half_dim = HEAD_DIM // 2
    scaled = grad_in * sin_t
    turned = jnp.concatenate([scaled[..., half_dim:], -scaled[..., :half_dim]], axis=-1)
    return grad_in * cos_t + turned


def block_fwd_bwd(x_rows, grad_out, gain_vec, w_query, b_query, w_key, b_key, w_value, b_value, w_out):
    batch_size, seq_len, model_width = x_rows.shape
    n_heads = w_query.shape[1] // HEAD_DIM
    kv_heads = w_key.shape[1] // HEAD_DIM
    q_group = n_heads // kv_heads
    score_scale = HEAD_DIM ** -0.5
    cos_t, sin_t = rope_tables(seq_len)
    x_full = x_rows.astype(jnp.float32)
    inv_rms = lax.rsqrt(jnp.mean(x_full * x_full, axis=-1, keepdims=True) + NORM_EPS)
    x_norm = x_full * inv_rms
    gain_f = gain_vec.astype(jnp.float32)
    hidden = (x_norm * gain_f).astype(jnp.bfloat16)
    q_lin = jnp.einsum("bli,io->blo", hidden, w_query, preferred_element_type=jnp.float32) + b_query.astype(jnp.float32)
    k_lin = jnp.einsum("bli,io->blo", hidden, w_key, preferred_element_type=jnp.float32) + b_key.astype(jnp.float32)
    v_lin = jnp.einsum("bli,io->blo", hidden, w_value, preferred_element_type=jnp.float32) + b_value.astype(jnp.float32)
    q_rot = rotate(q_lin.reshape(batch_size, seq_len, n_heads, HEAD_DIM), cos_t, sin_t).astype(jnp.bfloat16)
    q_rot = q_rot.reshape(batch_size, seq_len, kv_heads, q_group, HEAD_DIM)
    k_rot = rotate(k_lin.reshape(batch_size, seq_len, kv_heads, HEAD_DIM), cos_t, sin_t).astype(jnp.bfloat16)
    v_val = v_lin.astype(jnp.bfloat16).reshape(batch_size, seq_len, kv_heads, HEAD_DIM)
    scores = jnp.einsum("bqkgd,bskd->bkgqs", q_rot, k_rot, preferred_element_type=jnp.float32) * score_scale
    causal = jnp.arange(seq_len)[:, None] >= jnp.arange(seq_len)[None, :]
    scores = jnp.where(causal, scores, MASK_VALUE)
    prob_f = jax.nn.softmax(scores, axis=-1)
    prob_b = prob_f.astype(jnp.bfloat16)
    attn_out = jnp.einsum("bkgqs,bskd->bqkgd", prob_b, v_val, preferred_element_type=jnp.float32)
    attn_b = attn_out.astype(jnp.bfloat16).reshape(batch_size, seq_len, n_heads * HEAD_DIM)
    proj_out = jnp.einsum("bli,io->blo", attn_b, w_out, preferred_element_type=jnp.float32)
    block_out = (x_full + proj_out).astype(jnp.bfloat16)

    grad_wo = jnp.einsum("bli,blo->io", attn_b, grad_out, preferred_element_type=jnp.float32)
    d_attn = jnp.einsum("blo,io->bli", grad_out, w_out, preferred_element_type=jnp.float32)
    d_attn = d_attn.astype(jnp.bfloat16).reshape(batch_size, seq_len, kv_heads, q_group, HEAD_DIM)
    d_probs = jnp.einsum("bqkgd,bskd->bkgqs", d_attn, v_val, preferred_element_type=jnp.float32)
    d_val = jnp.einsum("bkgqs,bqkgd->bskd", prob_b, d_attn, preferred_element_type=jnp.float32)
    d_scores = prob_f * (d_probs - jnp.sum(d_probs * prob_f, axis=-1, keepdims=True))
    d_scores = (d_scores * score_scale).astype(jnp.bfloat16)
    d_qrot = jnp.einsum("bkgqs,bskd->bqkgd", d_scores, k_rot, preferred_element_type=jnp.float32)
    d_krot = jnp.einsum("bkgqs,bqkgd->bskd", d_scores, q_rot, preferred_element_type=jnp.float32)
    d_query = rotate_back(d_qrot.reshape(batch_size, seq_len, n_heads, HEAD_DIM), cos_t, sin_t)
    d_query = d_query.reshape(batch_size, seq_len, n_heads * HEAD_DIM)
    d_key = rotate_back(d_krot, cos_t, sin_t).reshape(batch_size, seq_len, kv_heads * HEAD_DIM)
    d_value = d_val.reshape(batch_size, seq_len, kv_heads * HEAD_DIM)
    grad_bq = jnp.sum(d_query, axis=(0, 1))
    grad_bk = jnp.sum(d_key, axis=(0, 1))
    grad_bv = jnp.sum(d_value, axis=(0, 1))
    dq_b = d_query.astype(jnp.bfloat16)
    dk_b = d_key.astype(jnp.bfloat16)
    dv_b = d_value.astype(jnp.bfloat16)
    grad_wq = jnp.einsum("bli,blo->io", hidden, dq_b, preferred_element_type=jnp.float32)
    grad_wk = jnp.einsum("bli,blo->io", hidden, dk_b, preferred_element_type=jnp.float32)
    grad_wv = jnp.einsum("bli,blo->io", hidden, dv_b, preferred_element_type=jnp.float32)
    d_hidden = jnp.einsum("blo,io->bli", dq_b, w_query, preferred_element_type=jnp.float32)
    d_hidden = d_hidden + jnp.einsum("blo,io->bli", dk_b, w_key, preferred_element_type=jnp.float32)
    d_hidden = d_hidden + jnp.einsum("blo,io->bli", dv_b, w_value, preferred_element_type=jnp.float32)
    grad_gain = jnp.sum(d_hidden * x_norm, axis=(0, 1))
    d_norm = d_hidden * gain_f
    d_x = grad_out.astype(jnp.float32) + inv_rms * (d_norm - x_norm * jnp.mean(d_norm * x_norm, axis=-1, keepdims=True))
    return block_out, d_x, (grad_gain, grad_wq, grad_bq, grad_wk, grad_bk, grad_wv, grad_bv, grad_wo)


def solution(mesh):
    row_spec = P("fsdp", None)
    vec_spec = P("fsdp")
    act_spec = P("fsdp", None, None)
    weight_specs = (vec_spec, row_spec, vec_spec, row_spec, vec_spec, row_spec, vec_spec, row_spec)
    in_specs = (row_spec, act_spec, row_spec) + weight_specs
    out_specs = (act_spec, row_spec) + weight_specs

    def device_step(tok_ids, grad_out, table_part, gain_part, wq_part, bq_part, wk_part, bk_part, wv_part, bv_part, wo_part):
        rows_dev = table_part.shape[0]
        model_width = table_part.shape[1]
        first_row = lax.axis_index("fsdp") * rows_dev
        all_ids = lax.all_gather(tok_ids, "fsdp")
        local_idx = all_ids - first_row
        is_owned = (local_idx >= 0) & (local_idx < rows_dev)
        looked = jnp.take(table_part, jnp.where(is_owned, local_idx, 0), axis=0)
        looked = jnp.where(is_owned[..., None], looked, jnp.zeros((), jnp.bfloat16))
        x_rows = lax.psum_scatter(looked, "fsdp", scatter_dimension=0)
        gain_full = lax.all_gather(gain_part, "fsdp", axis=0, tiled=True)
        wq_full = lax.all_gather(wq_part, "fsdp", axis=0, tiled=True)
        bq_full = lax.all_gather(bq_part, "fsdp", axis=0, tiled=True)
        wk_full = lax.all_gather(wk_part, "fsdp", axis=0, tiled=True)
        bk_full = lax.all_gather(bk_part, "fsdp", axis=0, tiled=True)
        wv_full = lax.all_gather(wv_part, "fsdp", axis=0, tiled=True)
        bv_full = lax.all_gather(bv_part, "fsdp", axis=0, tiled=True)
        wo_full = lax.all_gather(wo_part, "fsdp", axis=0, tiled=True)
        block_out, d_x, grad_list = block_fwd_bwd(x_rows, grad_out, gain_full, wq_full, bq_full, wk_full, bk_full, wv_full, bv_full, wo_full)
        all_dx = lax.all_gather(d_x, "fsdp")
        seg_idx = jnp.where(is_owned, local_idx, rows_dev)
        grad_part = jax.ops.segment_sum(all_dx.reshape(-1, model_width), seg_idx.reshape(-1), num_segments=rows_dev)
        reduced = tuple(lax.psum_scatter(grad_full, "fsdp", scatter_dimension=0, tiled=True) for grad_full in grad_list)
        return (block_out, grad_part.astype(jnp.bfloat16)) + reduced

    return jax.shard_map(device_step, mesh=mesh, in_specs=in_specs, out_specs=out_specs, check_vma=False)
```

profile of v0, /device:TPU:0, one launch (start us, length us, event | category | flops | bytes accessed | tf_op | source)
XLA Modules:
  0.0 2154.5 jit_solution(8752178806837243417)
XLA Ops:
  8.0 15.0 all-gather.2
  23.7 158.7 %gather_fusion = bf16[24576,1536]{1,0:T(8,128)(2,1)} fusion(bf16[9496,1536]{1,0:T(8,128)(2,1)} %param.13, s32[24576]{0:T(1024)S(1)} %broadcast_clamp_fusion.1), kind=kCustom, calls=%fused_computation | custom fusion | bytes 151093248 | tf_op jit(solution)/shard_map/jit(_take)/gather | solution.py:108
  182.4 49.4 %select_select_fusion = bf16[16,1,1536,1536]{3,2,1,0:T(8,128)(2,1)} fusion(bf16[16,1,1536,1536]{3,2,1,0:T(8,128)(2,1)} %bitcast.3, pred[16,1536]{1,0:T(8,128)(4,1)S(1)} %copy-done.28, pred[16,1536]{1,0:T(8,128)(4,1)S(1)} %copy-done.29), kind=kLoop, calls=%fused_computation.16 | loop fusion | flops 75497472 | bytes 151044096 | tf_op jit(solution)/shard_map/jit(_where)/select_n | solution.py:109
  233.7 32.2 %all-reduce.9 = (bf16[256]{0:T(256)(128)(2,1)S(1)}, bf16[1536]{0:T(1024)(128)(2,1)S(1)}, bf16[256]{0:T(256)(128)(2,1)S(1)}, bf16[1536]{0:T(1024)(128)(2,1)S(1)}) all-reduce(bf16[256]{0:T(256)(128)(2,1)S(1)} %dynamic-update-slice.1, bf16[1536]{0:T(1024)(128)(2,1)S(1)} %dynamic-update-slice, ...), channel_id=1, replica_groups=mesh['fsdp'=16] {'fsdp'}, use_global_device_ids=true, to_apply=%add.1 | all-reduce | flops 3584 | bytes 14336
  266.6 2.8 fusion.60
  269.4 14.0 all_gather.41
  283.4 12.8 all_gather.39
  296.3 2.2 iota_compare_fusion
  298.4 12.3 convolution_convert_fusion
  310.8 297.3 %reduce-scatter.6.cloned.1.call-done = bf16[1,1,1536,1536]{3,2,1,0:T(8,128)(2,1)} async-done(((bf16[16,1,1536,1536]{3,2,1,0:T(8,128)(2,1)}), bf16[1,1,1536,1536]{3,2,1,0:T(8,128)(2,1)}) %reduce-scatter.6.cloned.1.call-update) | async-done | bytes 4718608 | tf_op jit(solution)/shard_map/reduce_scatter | solution.py:110
  608.0 3.3 fusion.33
  611.4 4.2 convolution_add_fusion.3
  615.6 1.3 fusion.58
  616.9 30.0 %all-gather.7.cloned.1.call-done = bf16[1536,1536]{1,0:T(8,128)(2,1)} async-done(((bf16[96,1536]{1,0:T(8,128)(2,1)}), bf16[1536,1536]{1,0:T(8,128)(2,1)}) %all-gather.7.cloned.1.call-update) | async-done | bytes 4718608 | tf_op jit(solution)/shard_map/all_gather | solution.py:112
  646.9 11.9 convolution_add_fusion.2
  658.9 4.7 slice_negate_fusion.1
  663.6 1.9 copy-done.7
  666.0 8.1 fusion.37
  674.2 38.3 %fusion.11 = (f32[2,6,1536]{2,1,0:T(8,128)S(1)}, f32[2,1536,1536,6]{2,1,3,0:T(8,128)}) fusion(pred[1536,1536]{0,1:T(8,128)(4,1)S(1)} %copy-done.10, bf16[1536,2,128,1]{0,2,3,1:T(8,128)(2,1)S(1)} %fusion.57, bf16[1536,2,6,128]{0,3,2,1:T(8,128)(2,1)S(1)} %fusion.37), kind=kOutput, calls=%fused_computation.15 | convolution fusion | flops 7332673536 | bytes 121184256 | tf_op jit(solution)/shard_map/bqkgd,bskd->bkgqs/dot_general | solution.py:52
  712.5 35.0 %fusion.10 = f32[2,6,1536]{2,1,0:T(8,128)S(1)} fusion(f32[2,1536,1536,6]{2,1,3,0:T(8,128)} %get-tuple-element.42, f32[2,6,1536]{2,1,0:T(8,128)S(1)} %get-tuple-element.41, pred[1536,1536]{0,1:T(8,128)(4,1)S(1)} %copy-done.11), kind=kLoop, calls=%fused_computation.14 | loop fusion | flops 113227776 | bytes 115752960 | tf_op jit(solution)/shard_map/reduce_sum | solution.py:55
  747.5 46.4 %fusion.75 = (f32[2,128]{1,0:T(2,128)}, bf16[1,1536,2,128]{1,3,2,0:T(8,128)(2,1)}) fusion(bf16[1536,2,6,128]{0,3,2,1:T(8,128)(2,1)} %bitcast.237, f32[2,6,1536]{2,1,0:T(8,128)S(1)} %fusion.10, f32[2,6,1536]{2,1,0:T(8,128)S(1)} %get-tuple-element.41, f32[2,1536,1536,6]{2,1,3,0:T(8,128)} %get-tuple-element.42, pred[1536,1536]{0,1:T(8,128)(4,1)} %iota_compare_fusion), kind=kOutput, calls=%fused_computation.107 | convolution fusion | flops 7390101504 | bytes 121259008 | tf_op jit(solution)/shard_map/bkgqs,bqkgd->bskd/dot_general | solution.py:66
  794.0 2.7 fusion.54
  796.7 86.0 %fusion.5 = (f32[2,6,1536]{2,1,0:T(8,128)S(1)}, f32[2,1536,1536,6]{2,1,3,0:T(8,128)}) fusion(f32[2,6,1536]{2,1,0:T(8,128)S(1)} %fusion.10, f32[2,6,1536]{2,1,0:T(8,128)S(1)} %get-tuple-element.41, f32[2,1536,1536,6]{2,1,3,0:T(8,128)} %get-tuple-element.42, pred[1536,1536]{0,1:T(8,128)(4,1)} %iota_compare_fusion, bf16[1536,2,128,1]{0,2,3,1:T(8,128)(2,1)} %bitcast.239, ...), kind=kOutput, calls=%fused_computation.8 | convolution fusion | flops 7417608192 | bytes 234577920 | tf_op jit(solution)/shard_map/bqkgd,bskd->bkgqs/dot_general | solution.py:65
  882.6 89.1 %fusion.12 = bf16[2,6,1536,1536]{2,3,1,0:T(8,128)(2,1)} fusion(f32[2,1536,1536,6]{2,1,3,0:T(8,128)} %get-tuple-element.44, f32[2,6,1536]{2,1,0:T(8,128)S(1)} %get-tuple-element.43, f32[2,6,1536]{2,1,0:T(8,128)S(1)} %fusion.10, f32[2,6,1536]{2,1,0:T(8,128)S(1)} %get-tuple-element.41, f32[2,1536,1536,6]{2,1,3,0:T(8,128)} %get-tuple-element.42, ...), kind=kLoop, calls=%fused_computation.17 | loop fusion | flops 226492416 | bytes 285696000 | tf_op jit(solution)/shard_map/reshape.57
  971.8 26.2 %broadcast_multiply_fusion = (f32[1,1536,2,128]{1,3,2,0:T(8,128)S(1)}, f32[1,1536,2,128]{1,3,2,0:T(8,128)}) fusion(f32[1536,128]{0,1:T(8,128)S(1)} %copy-done.9, bf16[1536,2,6,128]{0,3,2,1:T(8,128)(2,1)} %copy-done, bf16[2,6,1536,1536]{2,3,1,0:T(8,128)(2,1)} %fusion.12), kind=kOutput, calls=%fused_computation.88 | convolution fusion | flops 7248150528 | bytes 65273856 | tf_op jit(solution)/shard_map/bkgqs,bqkgd->bskd/dot_general | solution.py:70
  997.9 24.0 %fusion.77 = f32[2,128,6,1536]{3,1,2,0:T(8,128)} fusion(bf16[1536,2,128,1]{0,2,3,1:T(8,128)(2,1)S(1)} %copy-done.18, bf16[2,6,1536,1536]{2,3,1,0:T(8,128)(2,1)} %fusion.12), kind=kOutput, calls=%fused_computation.109 | convolution fusion | flops 7247757312 | bytes 66846720 | tf_op jit(solution)/shard_map/bkgqs,bskd->bqkgd/dot_general | solution.py:69
  1021.9 1.3 fusion.76
  1023.2 8.6 bitcast_multiply_fusion.3
  1031.8 4.9 fusion.74
  1036.8 8.1 fusion.42
  1044.9 11.4 fusion.40
  1056.4 2.1 fusion.61
  1058.4 11.4 fusion.78
  1069.9 1.5 convolution_add_fusion.1
  1071.5 4.0 fusion.31
  1075.5 7.5 fusion.30
  1083.0 5.5 fusion.63
  1088.6 43.3 %fusion.48 = bf16[2,128,6,1536]{3,1,2,0:T(8,128)(2,1)} fusion(bf16[1536,2,128,1]{0,2,3,1:T(8,128)(2,1)} %bitcast.240, f32[2,6,1536]{2,1,0:T(8,128)S(1)} %fusion.10, f32[2,6,1536]{2,1,0:T(8,128)S(1)} %get-tuple-element.41, f32[2,1536,1536,6]{2,1,3,0:T(8,128)} %get-tuple-element.42, pred[1536,1536]{0,1:T(8,128)(4,1)S(1)} %copy-done.13), kind=kOutput, calls=%fused_computation.70 | convolution fusion | flops 7391674368 | bytes 121257984 | tf_op jit(solution)/shard_map/bkgqs,bskd->bqkgd/dot_general | solution.py:57
  1132.0 5.3 fusion.65
  1137.3 12.9 fusion.45
  1150.3 14.0 fusion.67
  1165.3 10.6 sort
  1176.0 7.6 fusion.38
  1183.6 33.2 %all-reduce.8 = (f32[1536]{0:T(1024)S(1)}, f32[1536]{0:T(1024)S(1)}, f32[256]{0:T(256)S(1)}, f32[256]{0:T(256)S(1)}) all-reduce(f32[1536]{0:T(1024)S(1)} %copy-done.40, f32[1536]{0:T(1024)S(1)} %reduce_sum.84, f32[256]{0:T(256)S(1)} %bitcast.233, f32[256]{0:T(256)S(1)} %bitcast.234), channel_id=5, replica_groups=mesh['fsdp'=16] {'fsdp'}, use_global_device_ids=true, to_apply=%region_8.9.clone | all-reduce | flops 3584 | bytes 28672
  1219.1 13.0 fusion.43
  1232.1 369.1 %all-gather.11.cloned.1.call-done = f32[16,1536,1536]{2,1,0:T(8,128)} async-done(((f32[1,1536,1536]{2,1,0:T(8,128)}), f32[16,1536,1536]{2,1,0:T(8,128)}) %all-gather.11.cloned.1.call-update) | async-done | bytes 150994960 | tf_op jit(solution)/shard_map/all_gather | solution.py:120
  1601.3 517.6 %scatter_custom_fusion = f32[9496,1536]{1,0:T(8,128)} fusion(s32[24576]{0:T(1024)S(1)} %get-tuple-element.10, f32[24576,1536]{1,0:T(8,128)} %bitcast.52, s32[24576]{0:T(1024)S(1)} %broadcast_clamp_fusion, f32[]{:T(128)} %constant.20.clone.1), kind=kCustom, calls=%fused_computation.3 | custom fusion | flops 37748736 | bytes 58343936 | tf_op jit(solution)/shard_map/scatter-add | solution.py:122
  2118.8 28.2 %convert_element_type.184 = bf16[9496,1536]{1,0:T(8,128)(2,1)} convert(f32[9496,1536]{1,0:T(8,128)} %scatter_custom_fusion) | non-fusion elementwise | flops 14585856 | bytes 87515136 | tf_op jit(solution)/shard_map/convert_element_type | solution.py:124
  (157 shorter events, 8.2 us)
Async XLA Ops:
  7.2 291.2 %all-gather.9.cloned.1.call-start = ((), (), s32[]{:S(2)}) async-start(), calls=%async_computation.7 | async-start | bytes 5013504 | tf_op jit(solution)/shard_map/all_gather | solution.py:118
  7.9 600.1 %reduce-scatter.6.cloned.1.call-start = ((), (), s32[]{:S(2)}) async-start(), calls=%async_computation.5 | async-start | bytes 80216064 | tf_op jit(solution)/shard_map/reduce_scatter | solution.py:110
  23.0 159.4 %copy-start.25 = (s32[16,1,1536]{2,1,0:T(1,128)}, s32[16,1,1536]{2,1,0:T(1,128)S(1)}, u32[]{:S(2)}) copy-start(s32[16,1,1536]{2,1,0:T(1,128)S(1)} %all-gather.2) | copy-start | bytes 294916
  23.7 158.7 %copy-start.28 = (pred[16,1536]{1,0:T(8,128)(4,1)S(1)}, pred[16,1536]{1,0:T(8,128)(4,1)}, u32[]{:S(2)}) copy-start(pred[16,1536]{1,0:T(8,128)(4,1)} %get-tuple-element.22) | copy-start | bytes 73732
  23.7 158.7 %copy-start.29 = (pred[16,1536]{1,0:T(8,128)(4,1)S(1)}, pred[16,1536]{1,0:T(8,128)(4,1)}, u32[]{:S(2)}) copy-start(pred[16,1536]{1,0:T(8,128)(4,1)} %get-tuple-element.40) | copy-start | bytes 73732
  231.8 37.6 %copy-start.38 = (bf16[96,256]{1,0:T(8,128)(2,1)S(1)}, bf16[96,256]{1,0:T(8,128)(2,1)}, u32[]{:S(2)}) copy-start(bf16[96,256]{1,0:T(8,128)(2,1)} %param.17) | copy-start | bytes 147460
  231.8 51.6 %copy-start.39 = (bf16[96,256]{1,0:T(8,128)(2,1)S(1)}, bf16[96,256]{1,0:T(8,128)(2,1)}, u32[]{:S(2)}) copy-start(bf16[96,256]{1,0:T(8,128)(2,1)} %param.19) | copy-start | bytes 147460
  231.9 415.1 %all-gather.7.cloned.1.call-start = ((), (), s32[]{:S(2)}) async-start(), calls=%async_computation.6 | async-start | bytes 5013504 | tf_op jit(solution)/shard_map/all_gather | solution.py:112
  232.6 1368.7 %all-gather.11.cloned.1.call-start = ((), (), s32[]{:S(2)}) async-start(), calls=%async_computation.12 | async-start | bytes 160432128 | tf_op jit(solution)/shard_map/all_gather | solution.py:120
  266.5 380.5 %copy-start.30 = (f32[1536]{0:T(1024)}, f32[1536]{0:T(1024)S(1)}, u32[]{:S(2)}) copy-start(f32[1536]{0:T(1024)S(1)} %convert_element_type.162) | copy-start | bytes 18436
  269.4 396.6 %copy-start.4 = (f32[1536,128]{0,1:T(8,128)}, f32[1536,128]{0,1:T(8,128)S(1)}, u32[]{:S(2)}) copy-start(f32[1536,128]{0,1:T(8,128)S(1)} %get-tuple-element.38) | copy-start | bytes 2359300
  269.4 396.6 %copy-start.8 = (f32[1536,128]{0,1:T(8,128)}, f32[1536,128]{0,1:T(8,128)S(1)}, u32[]{:S(2)}) copy-start(f32[1536,128]{0,1:T(8,128)S(1)} %get-tuple-element.39) | copy-start | bytes 2359300
  611.4 35.6 %copy-start.34 = (f32[1536]{0:T(1024)}, f32[1536]{0:T(1024)S(1)}, u32[]{:S(2)}) copy-start(f32[1536]{0:T(1024)S(1)} %add_rsqrt_fusion) | copy-start | bytes 18436
  658.9 6.6 copy-start.7
  666.0 8.2 copy-start.17
  666.0 8.2 copy-start.10
  674.1 38.4 %copy-start = (bf16[1536,2,6,128]{0,3,2,1:T(8,128)(2,1)}, bf16[1536,2,6,128]{0,3,2,1:T(8,128)(2,1)S(1)}, u32[]{:S(2)}) copy-start(bf16[1536,2,6,128]{0,3,2,1:T(8,128)(2,1)S(1)} %fusion.37) | copy-start | bytes 14155780
  674.2 38.4 %copy-start.11 = (pred[1536,1536]{0,1:T(8,128)(4,1)S(1)}, pred[1536,1536]{0,1:T(8,128)(4,1)}, u32[]{:S(2)}) copy-start(pred[1536,1536]{0,1:T(8,128)(4,1)} %iota_compare_fusion) | copy-start | bytes 7077892
  747.5 46.5 %copy-start.1 = (bf16[1,1,1536,1536]{3,2,1,0:T(8,128)(2,1)S(1)}, bf16[1,1,1536,1536]{3,2,1,0:T(8,128)(2,1)}, u32[]{:S(2)}) copy-start(bf16[1,1,1536,1536]{3,2,1,0:T(8,128)(2,1)} %reduce-scatter.6.cloned.1.call-done) | copy-start | bytes 14155780
  747.5 46.5 %copy-start.19 = (bf16[1536,256]{1,0:T(8,128)(2,1)S(1)}, bf16[1536,256]{1,0:T(8,128)(2,1)}, u32[]{:S(2)}) copy-start(bf16[1536,256]{1,0:T(8,128)(2,1)} %all_gather.39) | copy-start | bytes 2359300
  747.5 46.4 %copy-start.31 = (f32[1536]{0:T(1024)S(1)}, f32[1536]{0:T(1024)}, u32[]{:S(2)}) copy-start(f32[1536]{0:T(1024)} %copy-done.30) | copy-start | bytes 18436
  747.5 46.4 %copy-start.35 = (f32[1536]{0:T(1024)S(1)}, f32[1536]{0:T(1024)}, u32[]{:S(2)}) copy-start(f32[1536]{0:T(1024)} %copy-done.34) | copy-start | bytes 18436
  747.5 46.4 %copy-start.47 = (f32[256]{0:T(256)S(1)}, f32[256]{0:T(256)}, u32[]{:S(2)}) copy-start(f32[256]{0:T(256)} %convert_element_type.164) | copy-start | bytes 3076
  796.7 86.0 %copy-start.12 = (pred[1536,1536]{0,1:T(8,128)(4,1)S(1)}, pred[1536,1536]{0,1:T(8,128)(4,1)}, u32[]{:S(2)}) copy-start(pred[1536,1536]{0,1:T(8,128)(4,1)} %iota_compare_fusion) | copy-start | bytes 7077892
  882.6 89.1 %copy-start.9 = (f32[1536,128]{0,1:T(8,128)S(1)}, f32[1536,128]{0,1:T(8,128)}, u32[]{:S(2)}) copy-start(f32[1536,128]{0,1:T(8,128)} %copy-done.8) | copy-start | bytes 2359300
  971.8 26.2 %copy-start.18 = (bf16[1536,2,128,1]{0,2,3,1:T(8,128)(2,1)S(1)}, bf16[1536,2,128,1]{0,2,3,1:T(8,128)(2,1)}, u32[]{:S(2)}) copy-start(bf16[1536,2,128,1]{0,2,3,1:T(8,128)(2,1)} %copy-done.17) | copy-start | bytes 2359300
  1023.2 13.6 slice-start
  1023.2 13.6 slice-start.1
  1036.7 8.2 copy-start.2
  1036.7 8.2 copy-start.3
  1044.9 11.4 copy-start.5
  1044.9 11.4 copy-start.14
  1044.9 11.4 copy-start.21
  1056.3 15.1 slice-start.3
  1058.4 11.4 copy-start.15
  1058.4 11.5 copy-start.24
  1058.4 13.0 slice-start.4
  1083.0 1064.1 %reduce-scatter.12.cloned.1.call-start = ((), (), s32[]{:S(2)}) async-start(), calls=%async_computation.10 | async-start | bytes 1671168 | tf_op jit(solution)/shard_map/reduce_scatter | solution.py:123
  1088.6 1058.6 %reduce-scatter.10.cloned.1.call-start = ((), (), s32[]{:S(2)}) async-start(), calls=%async_computation.9 | async-start | bytes 1671168 | tf_op jit(solution)/shard_map/reduce_scatter | solution.py:123
  1088.6 43.3 %copy-start.16 = (bf16[1,1536,2,128]{1,3,2,0:T(8,128)(2,1)S(1)}, bf16[1,1536,2,128]{1,3,2,0:T(8,128)(2,1)}, u32[]{:S(2)}) copy-start(bf16[1,1536,2,128]{1,3,2,0:T(8,128)(2,1)} %copy-done.15) | copy-start | bytes 2359300
  1088.6 43.3 %copy-start.33 = (f32[1536]{0:T(1024)S(1)}, f32[1536]{0:T(1024)}, u32[]{:S(2)}) copy-start(f32[1536]{0:T(1024)} %copy-done.30) | copy-start | bytes 18436
  1088.6 43.3 %copy-start.37 = (f32[1536]{0:T(1024)S(1)}, f32[1536]{0:T(1024)}, u32[]{:S(2)}) copy-start(f32[1536]{0:T(1024)} %copy-done.34) | copy-start | bytes 18436
  1137.3 1009.8 %reduce-scatter.14.cloned.1.call-start = ((), (), s32[]{:S(2)}) async-start(), calls=%async_computation.11 | async-start | bytes 10027008 | tf_op jit(solution)/shard_map/reduce_scatter | solution.py:123
  1150.3 996.9 %reduce-scatter.8.cloned.1.call-start = ((), (), s32[]{:S(2)}) async-start(), calls=%async_computation.8 | async-start | bytes 10027008 | tf_op jit(solution)/shard_map/reduce_scatter | solution.py:123
  1164.4 11.6 copy-start.6
  1175.9 7.6 copy-start.40
  1176.0 7.6 copy-start.41
  1176.0 7.6 copy-start.42
  (13 other events, 35.8 us)
Sparse Core Ops, SparseCore 0:
  10.2 39.4 all-gather.8
  232.0 376.0 reduce-scatter.5
  610.3 36.6 all-gather.6
  1083.1 518.1 all-gather.10
  1605.7 49.3 reduce-scatter.11
  1659.5 49.3 reduce-scatter.9
  1714.1 79.4 reduce-scatter.13
  1798.8 79.4 reduce-scatter.7
where the time goes:
time: 2170 us; the launch traced here: 2150 us
  other arithmetic  806 us (37%)
  waiting for transfers between devices  698 us (32%)
  matrix products  363 us (17%)
  local copies, waits for them, and re-layouts  165 us (8%)
  blocking collectives  107 us (5%)
    scatter-add x3, other arithmetic, device_step(): jax.ops.segment_sum(all_dx.reshape(-1, model_width), seg_idx.reshape(-1),...  528 us
    all_gather x1, waiting for transfers between devices, device_step(): all_dx = lax.all_gather(d_x, 'fsdp')  369 us
    reduce_scatter x1, waiting for transfers between devices, device_step(): x_rows = lax.psum_scatter(looked, 'fsdp', scatter_dimension=0)  297 us
    gather x1, local copies, waits for them, and re-layouts, device_step(): looked = jnp.take(table_part, jnp.where(is_owned, local_idx, 0), axis=0)  159 us
    another operation x1, other arithmetic  89.1 us
    dot_general x1, matrix products, block_fwd_bwd(): jnp.einsum('bqkgd,bskd->bkgqs', d_attn, v_val, preferred_element_type=jnp...  86 us
    unnamed x2, blocking collectives  65.4 us
    select_n x1, other arithmetic, device_step(): looked = jnp.where(is_owned[..., None], looked, jnp.zeros((), jnp.bfloat16))  49.4 us
  transfers between devices with their start and end apart: 8, of which 3 were waited for; matrix products, arithmetic and copies ran while one was open for 42% of the time, Pallas kernels for 0%

commit v1 on v0

v1 whole, which is shorter than its diff:
```python
import functools

import jax
import jax.numpy as jnp
from jax import lax
from jax.experimental import pallas as pl
from jax.experimental.pallas import tpu as pltpu
from jax.sharding import PartitionSpec as P

HEAD_DIM = 128
ROPE_THETA = 1.0e6
NORM_EPS = 1e-6
MASK_VALUE = -1e30
N_DEV = 16
HOT_IDS = 4096
HOT_ROWS = HOT_IDS // N_DEV
HOT_GROUPS = HOT_IDS // (N_DEV * 8)
CAP = 144
Q_BLOCK = 256
ROW_BLOCK = 256
F32 = jnp.float32
BF16 = jnp.bfloat16
MESH_ID = pl.DeviceIdType.MESH
VMEM_LIMIT = 60 * 1024 * 1024


def rope_tables(seq_len):
    half_dim = HEAD_DIM // 2
    inv_freq = jnp.power(ROPE_THETA, -(jnp.arange(half_dim, dtype=F32) * 2.0 / HEAD_DIM))
    angles = jnp.arange(seq_len, dtype=F32)[:, None] * inv_freq[None, :]
    cos_h, sin_h = jnp.cos(angles), jnp.sin(angles)
    return jnp.concatenate([cos_h, cos_h], axis=-1), jnp.concatenate([-sin_h, sin_h], axis=-1)


def all_barrier():
    me = lax.axis_index("fsdp")
    barrier = pltpu.get_barrier_semaphore()
    for k in range(1, N_DEV):
        pl.semaphore_signal(barrier, inc=1, device_id=(lax.rem(me + k, N_DEV),), device_id_type=MESH_ID)
    pl.semaphore_wait(barrier, N_DEV - 1)


def head_exchange_kernel(table_ref, req_ref, small_ref, hot_ref, reqs_ref, smalls_ref, bounce, send_q, recv_q, send_s, recv_s, send_h, recv_h, local):
    me = lax.axis_index("fsdp")
    all_barrier()
    copies = []
    for k in range(1, N_DEV):
        to = lax.rem(me + k, N_DEV)
        copies.append(pltpu.make_async_remote_copy(req_ref.at[to], reqs_ref.at[me], send_q.at[k], recv_q.at[k], (to,), MESH_ID))
        copies.append(pltpu.make_async_remote_copy(small_ref, smalls_ref.at[me], send_s.at[k], recv_s.at[k], (to,), MESH_ID))
    for copy in copies:
        copy.start()

    @pl.when(me == 0)
    def _():
        hot_copies = []
        for k in range(1, N_DEV):
            hot_copies.append(pltpu.make_async_remote_copy(table_ref.at[pl.ds(0, HOT_GROUPS), k], hot_ref, send_h.at[k], recv_h, (k,), MESH_ID))
        for copy in hot_copies:
            copy.start()
        mine = pltpu.make_async_copy(table_ref.at[pl.ds(0, HOT_GROUPS), 0], bounce, local)
        mine.start()
        mine.wait()
        mine = pltpu.make_async_copy(bounce, hot_ref, local)
        mine.start()
        mine.wait()
        for copy in hot_copies:
            copy.wait_send()

    reqs_ref[me] = req_ref[me]
    smalls_ref[me] = small_ref[...]

    @pl.when(me != 0)
    def _():
        pltpu.make_async_remote_copy(table_ref.at[pl.ds(0, HOT_GROUPS), 0], hot_ref, send_h.at[0], recv_h, (0,), MESH_ID).wait_recv()

    for copy in copies:
        copy.wait()


def head_exchange(table_part, requests, small_vec):
    rows_dev, width = table_part.shape
    table_view = table_part[:HOT_IDS].reshape(HOT_GROUPS, N_DEV, 8, width)
    any_spec = pl.BlockSpec(memory_space=pl.ANY)
    vmem_spec = pl.BlockSpec(memory_space=pltpu.VMEM)
    return pl.pallas_call(
        head_exchange_kernel,
        out_shape=(
            jax.ShapeDtypeStruct((HOT_GROUPS, 8, width), BF16),
            jax.ShapeDtypeStruct((N_DEV,) + requests.shape[1:], jnp.int32),
            jax.ShapeDtypeStruct((N_DEV,) + small_vec.shape, F32),
        ),
        in_specs=[any_spec, vmem_spec, vmem_spec],
        out_specs=(any_spec, vmem_spec, vmem_spec),
        scratch_shapes=[pltpu.VMEM((HOT_GROUPS, 8, width), BF16)]
        + [pltpu.SemaphoreType.DMA((N_DEV,))] * 5
        + [pltpu.SemaphoreType.DMA, pltpu.SemaphoreType.DMA],
        compiler_params=pltpu.CompilerParams(collective_id=1, has_side_effects=True),
        name="head_exchange",
    )(table_view, requests, small_vec)


def hot_return_kernel(sums_ref, out_ref, send_h, recv_h, local, bounce):
    me = lax.axis_index("fsdp")
    all_barrier()

    @pl.when(me == 0)
    def _():
        mine = pltpu.make_async_copy(sums_ref, bounce, local)
        mine.start()
        mine.wait()
        mine = pltpu.make_async_copy(bounce, out_ref.at[:, 0], local)
        mine.start()
        mine.wait()
        for k in range(1, N_DEV):
            pltpu.make_async_remote_copy(sums_ref, out_ref.at[:, k], send_h, recv_h.at[k], (k,), MESH_ID).wait_recv()

    @pl.when(me != 0)
    def _():
        copy = pltpu.make_async_remote_copy(sums_ref, out_ref.at[:, me], send_h, recv_h.at[me], (0,), MESH_ID)
        copy.start()
        copy.wait_send()


def hot_return(hot_sums):
    groups, _, width = hot_sums.shape
    any_spec = pl.BlockSpec(memory_space=pl.ANY)
    return pl.pallas_call(
        hot_return_kernel,
        out_shape=jax.ShapeDtypeStruct((groups, N_DEV, 8, width), BF16),
        in_specs=[any_spec],
        out_specs=any_spec,
        scratch_shapes=[
            pltpu.SemaphoreType.DMA,
            pltpu.SemaphoreType.DMA((N_DEV,)),
            pltpu.SemaphoreType.DMA,
            pltpu.VMEM((groups, 8, width), BF16),
        ],
        compiler_params=pltpu.CompilerParams(collective_id=2, has_side_effects=True),
        name="hot_return",
    )(hot_sums)


def qkv_kernel(x_ref, w_ref, gain_ref, bias_ref, cos_ref, sin_ref, hidden_ref, qkv_ref):
    x_f = x_ref[...].astype(F32)
    inv_rms = lax.rsqrt(jnp.mean(x_f * x_f, axis=-1, keepdims=True) + NORM_EPS)
    hidden = (x_f * inv_rms * gain_ref[...]).astype(BF16)
    hidden_ref[...] = hidden
    cos_t, sin_t = cos_ref[...], sin_ref[...]
    n_rot = qkv_ref.shape[1] // HEAD_DIM
    for c in range(n_rot // 2):
        cols = pl.ds(c * 2 * HEAD_DIM, 2 * HEAD_DIM)
        lin = jnp.dot(hidden, w_ref[:, cols], preferred_element_type=F32) + bias_ref[:, cols]
        for j in range(2):
            head = 2 * c + j
            vec = lin[:, j * HEAD_DIM : (j + 1) * HEAD_DIM]
            if head < 12 or head in (12, 14):
                vec = vec * cos_t + pltpu.roll(vec, HEAD_DIM // 2, 1) * sin_t
            qkv_ref[:, head * HEAD_DIM : (head + 1) * HEAD_DIM] = vec.astype(BF16)


def qkv_proj(x_rows, w_all, gain_row, bias_row, cos_t, sin_t):
    seq_len, width = x_rows.shape
    cols = bias_row.shape[1]
    return pl.pallas_call(
        qkv_kernel,
        grid=(seq_len // ROW_BLOCK,),
        out_shape=(jax.ShapeDtypeStruct((seq_len, width), BF16), jax.ShapeDtypeStruct((seq_len, cols), BF16)),
        in_specs=[
            pl.BlockSpec((ROW_BLOCK, width), lambda i: (i, 0)),
            pl.BlockSpec((width, cols), lambda i: (0, 0)),
            pl.BlockSpec((1, width), lambda i: (0, 0)),
            pl.BlockSpec((1, cols), lambda i: (0, 0)),
            pl.BlockSpec((ROW_BLOCK, HEAD_DIM), lambda i: (i, 0)),
            pl.BlockSpec((ROW_BLOCK, HEAD_DIM), lambda i: (i, 0)),
        ],
        out_specs=(pl.BlockSpec((ROW_BLOCK, width), lambda i: (i, 0)), pl.BlockSpec((ROW_BLOCK, cols), lambda i: (i, 0))),
        compiler_params=pltpu.CompilerParams(vmem_limit_bytes=VMEM_LIMIT),
        cost_estimate=pl.CostEstimate(flops=2 * seq_len * width * cols, bytes_accessed=20_000_000, transcendentals=0),
        name="qkv_proj",
    )(x_rows, w_all, gain_row, bias_row, cos_t, sin_t)


def attention_kernel(q_ref, k_ref, v_ref, do_ref, cosq_ref, sinq_ref, cosk_ref, sink_ref, o_ref, dq_ref, dkv_ref, dbq_ref, dbkv_ref, dk_acc, dv_acc, kt_ref, vt_ref):
    h_step, q_step = pl.program_id(1), pl.program_id(2)
    n_q = pl.num_programs(2)
    scale = HEAD_DIM**-0.5

    @pl.when((h_step == 0) & (q_step == 0))
    def _():
        dk_acc[...] = jnp.zeros_like(dk_acc)
        dv_acc[...] = jnp.zeros_like(dv_acc)
        kt_ref[...] = k_ref[...].T
        vt_ref[...] = v_ref[...].T

    q_blk, do_blk = q_ref[...], do_ref[...]
    last_dims = (((1,), (1,)), ((), ()))

    def step(length):
        s_t = lax.dot_general(k_ref[:length, :], q_blk, last_dims, preferred_element_type=F32) * scale
        key_pos = lax.broadcasted_iota(jnp.int32, (Q_BLOCK, Q_BLOCK), 0)
        query_pos = lax.broadcasted_iota(jnp.int32, (Q_BLOCK, Q_BLOCK), 1)
        diag = jnp.where(query_pos >= key_pos, s_t[length - Q_BLOCK :], MASK_VALUE)
        s_t = diag if length == Q_BLOCK else jnp.concatenate([s_t[: length - Q_BLOCK], diag], axis=0)
        top = jnp.max(s_t, axis=0, keepdims=True)
        e_t = jnp.exp(s_t - top)
        p_t = e_t * (1.0 / jnp.sum(e_t, axis=0, keepdims=True))
        p_b = p_t.astype(BF16)
        o_ref[...] = jnp.dot(vt_ref[:, :length], p_b, preferred_element_type=F32).T.astype(BF16)
        dp_t = lax.dot_general(v_ref[:length, :], do_blk, last_dims, preferred_element_type=F32)
        delta = jnp.sum(dp_t * p_t, axis=0, keepdims=True)
        ds_b = (p_t * (dp_t - delta) * scale).astype(BF16)
        dv_acc[:length, :] += jnp.dot(p_b, do_blk, preferred_element_type=F32)
        dk_acc[:length, :] += jnp.dot(ds_b, q_blk, preferred_element_type=F32)
        dq = jnp.dot(kt_ref[:, :length], ds_b, preferred_element_type=F32).T
        dq = dq * cosq_ref[...] - pltpu.roll(dq, HEAD_DIM // 2, 1) * sinq_ref[...]
        dq_ref[...] = dq.astype(BF16)
        part = jnp.sum(dq, axis=0, keepdims=True)
        dbq_ref[0] = part if length == Q_BLOCK else dbq_ref[0] + part

    for i in range(k_ref.shape[0] // Q_BLOCK):
        pl.when(q_step == i)(functools.partial(step, (i + 1) * Q_BLOCK))

    @pl.when((h_step == pl.num_programs(1) - 1) & (q_step == n_q - 1))
    def _():
        dk = dk_acc[...]
        dk = dk * cosk_ref[...] - pltpu.roll(dk, HEAD_DIM // 2, 1) * sink_ref[...]
        dv = dv_acc[...]
        dkv_ref[:, :HEAD_DIM] = dk.astype(BF16)
        dkv_ref[:, HEAD_DIM:] = dv.astype(BF16)
        dbkv_ref[0, :, :HEAD_DIM] = jnp.sum(dk, axis=0, keepdims=True)
        dbkv_ref[0, :, HEAD_DIM:] = jnp.sum(dv, axis=0, keepdims=True)


def attention(qkv, d_attn, cos_t, sin_t, n_heads, kv_heads):
    seq_len = qkv.shape[0]
    group = n_heads // kv_heads
    grid = (kv_heads, group, seq_len // Q_BLOCK)
    head_blk = pl.BlockSpec((Q_BLOCK, HEAD_DIM), lambda g, h, i: (i, g * group + h))
    rope_q = pl.BlockSpec((Q_BLOCK, HEAD_DIM), lambda g, h, i: (i, 0))
    rope_k = pl.BlockSpec((seq_len, HEAD_DIM), lambda g, h, i: (0, 0))
    return pl.pallas_call(
        attention_kernel,
        grid=grid,
        out_shape=(
            jax.ShapeDtypeStruct((seq_len, n_heads * HEAD_DIM), BF16),
            jax.ShapeDtypeStruct((seq_len, n_heads * HEAD_DIM), BF16),
            jax.ShapeDtypeStruct((seq_len, 2 * kv_heads * HEAD_DIM), BF16),
            jax.ShapeDtypeStruct((n_heads, 1, HEAD_DIM), F32),
            jax.ShapeDtypeStruct((kv_heads, 1, 2 * HEAD_DIM), F32),
        ),
        in_specs=[
            head_blk,
            pl.BlockSpec((seq_len, HEAD_DIM), lambda g, h, i: (0, n_heads + 2 * g)),
            pl.BlockSpec((seq_len, HEAD_DIM), lambda g, h, i: (0, n_heads + 2 * g + 1)),
            head_blk,
            rope_q,
            rope_q,
            rope_k,
            rope_k,
        ],
        out_specs=(
            head_blk,
            head_blk,
            pl.BlockSpec((seq_len, 2 * HEAD_DIM), lambda g, h, i: (0, g)),
            pl.BlockSpec((1, 1, HEAD_DIM), lambda g, h, i: (g * group + h, 0, 0)),
            pl.BlockSpec((1, 1, 2 * HEAD_DIM), lambda g, h, i: (g, 0, 0)),
        ),
        scratch_shapes=[
            pltpu.VMEM((seq_len, HEAD_DIM), F32),
            pltpu.VMEM((seq_len, HEAD_DIM), F32),
            pltpu.VMEM((HEAD_DIM, seq_len), BF16),
            pltpu.VMEM((HEAD_DIM, seq_len), BF16),
        ],
        compiler_params=pltpu.CompilerParams(vmem_limit_bytes=VMEM_LIMIT),
        cost_estimate=pl.CostEstimate(flops=6 * 2 * n_heads * seq_len * seq_len * HEAD_DIM, bytes_accessed=25_000_000, transcendentals=0),
        name="attention",
    )(qkv, qkv, qkv, d_attn, cos_t, sin_t, cos_t, sin_t)


def dx_kernel(dq_ref, dkv_ref, w_ref, x_ref, go_ref, gain_ref, dx_ref, dqkv_ref, dgain_ref):
    q_cols = dq_ref.shape[1]
    last_dims = (((1,), (1,)), ((), ()))
    dq, dkv = dq_ref[...], dkv_ref[...]
    dqkv_ref[:, :q_cols] = dq
    dqkv_ref[:, q_cols:] = dkv
    d_hidden = lax.dot_general(dq, w_ref[:, :q_cols], last_dims, preferred_element_type=F32)
    d_hidden += lax.dot_general(dkv, w_ref[:, q_cols:], last_dims, preferred_element_type=F32)
    x_f = x_ref[...].astype(F32)
    inv_rms = lax.rsqrt(jnp.mean(x_f * x_f, axis=-1, keepdims=True) + NORM_EPS)
    x_norm = x_f * inv_rms
    part = jnp.sum(d_hidden * x_norm, axis=0, keepdims=True)
    first = pl.program_id(0) == 0
    dgain_ref[...] = jnp.where(first, part, dgain_ref[...] + part)
    d_norm = d_hidden * gain_ref[...]
    d_x = inv_rms * (d_norm - x_norm * jnp.mean(d_norm * x_norm, axis=-1, keepdims=True))
    dx_ref[...] = go_ref[...].astype(F32) + d_x


def input_grad(dq_b, dkv_b, w_all, x_rows, grad_out, gain_row):
    seq_len, width = x_rows.shape
    q_cols, kv_cols = dq_b.shape[1], dkv_b.shape[1]
    cols = q_cols + kv_cols
    row_blk = pl.BlockSpec((ROW_BLOCK, width), lambda i: (i, 0))
    return pl.pallas_call(
        dx_kernel,
        grid=(seq_len // ROW_BLOCK,),
        out_shape=(
            jax.ShapeDtypeStruct((seq_len, width), F32),
            jax.ShapeDtypeStruct((seq_len, cols), BF16),
            jax.ShapeDtypeStruct((1, width), F32),
        ),
        in_specs=[
            pl.BlockSpec((ROW_BLOCK, q_cols), lambda i: (i, 0)),
            pl.BlockSpec((ROW_BLOCK, kv_cols), lambda i: (i, 0)),
            pl.BlockSpec((width, cols), lambda i: (0, 0)),
            row_blk,
            row_blk,
            pl.BlockSpec((1, width), lambda i: (0, 0)),
        ],
        out_specs=(row_blk, pl.BlockSpec((ROW_BLOCK, cols), lambda i: (i, 0)), pl.BlockSpec((1, width), lambda i: (0, 0))),
        compiler_params=pltpu.CompilerParams(vmem_limit_bytes=VMEM_LIMIT),
        cost_estimate=pl.CostEstimate(flops=2 * seq_len * width * cols, bytes_accessed=40_000_000, transcendentals=0),
        name="input_grad",
    )(dq_b, dkv_b, w_all, x_rows, grad_out, gain_row)


def routing(ids, rows_dev):
    agg = jnp.where(ids < HOT_IDS, (ids // 8) % N_DEV, ids // rows_dev)
    pos = jnp.arange(ids.shape[0], dtype=jnp.int32)
    same = ids[:, None] == ids[None, :]
    first = ~jnp.any(same & (pos[:, None] < pos[None, :]), axis=0)
    lower = first[:, None] & (agg[:, None] == agg[None, :]) & (ids[:, None] < ids[None, :])
    slot = jnp.sum(lower.astype(jnp.int32), axis=0)
    place = jnp.where(first & (slot < CAP), agg * CAP + slot, N_DEV * CAP)
    slots = jnp.arange(N_DEV * CAP, dtype=jnp.int32)
    requests = jnp.sum(jnp.where(place[:, None] == slots[None, :], ids[:, None] + 1, 0), axis=0)
    return agg, slot, requests.reshape(N_DEV, 1, CAP), jnp.max(slot) + 1


def solution(mesh):
    row_spec = P("fsdp", None)
    vec_spec = P("fsdp")
    act_spec = P("fsdp", None, None)
    weight_specs = (vec_spec, row_spec, vec_spec, row_spec, vec_spec, row_spec, vec_spec, row_spec)
    in_specs = (row_spec, act_spec, row_spec) + weight_specs
    out_specs = (act_spec, row_spec) + weight_specs

    def device_step(tok_ids, grad_out, table_part, gain_part, wq_part, bq_part, wk_part, bk_part, wv_part, bv_part, wo_part):
        rows_dev, width = table_part.shape
        q_cols, kv_cols = wq_part.shape[1], wk_part.shape[1]
        n_heads, kv_heads = q_cols // HEAD_DIM, kv_cols // HEAD_DIM
        seq_len = tok_ids.shape[1]
        me = lax.axis_index("fsdp")
        first_row = me * rows_dev
        ids = tok_ids[0]
        grad_seq = grad_out[0]

        def kv_order(k_arr, v_arr):
            parts = []
            for g in range(kv_heads):
                parts += [k_arr[..., g * HEAD_DIM : (g + 1) * HEAD_DIM], v_arr[..., g * HEAD_DIM : (g + 1) * HEAD_DIM]]
            return parts

        wqkv_full = lax.all_gather(jnp.concatenate([wq_part] + kv_order(wk_part, wv_part), axis=1), "fsdp", axis=0, tiled=True)
        wo_full = lax.all_gather(wo_part, "fsdp", axis=0, tiled=True)
        cos_t, sin_t = rope_tables(seq_len)

        agg, slot, requests, most = routing(ids, rows_dev)
        small = jnp.concatenate([gain_part, bq_part, bk_part, bv_part]).astype(F32)
        n_small = small.shape[0]
        small = jnp.concatenate([small, most.astype(F32)[None], jnp.zeros((256 - n_small - 1,), F32)])[None]
        hot_rows, wanted, smalls = head_exchange(table_part, requests, small)
        smalls = smalls[:, 0]
        n_g, n_q, n_kv = gain_part.shape[0], bq_part.shape[0], bk_part.shape[0]
        gain_row = smalls[:, :n_g].reshape(1, width)
        bq_full = smalls[:, n_g : n_g + n_q].reshape(q_cols)
        bk_full = smalls[:, n_g + n_q : n_g + n_q + n_kv].reshape(kv_cols)
        bv_full = smalls[:, n_g + n_q + n_kv : n_small].reshape(kv_cols)
        bias_row = jnp.concatenate([bq_full] + kv_order(bk_full, bv_full))[None]
        fits = jnp.max(smalls[:, n_small]) <= CAP

        wanted = wanted.reshape(N_DEV * CAP) - 1
        asked = wanted >= 0
        is_hot = wanted < HOT_IDS
        hot_idx = jnp.where(asked & is_hot, (wanted // (8 * N_DEV)) * 8 + wanted % 8, 0)
        cold_idx = jnp.where(asked & ~is_hot, wanted - first_row, 0)
        token_place = agg * CAP + jnp.minimum(slot, CAP - 1)

        def owned_index():
            all_ids = lax.all_gather(ids, "fsdp")
            local_idx = all_ids - first_row
            return local_idx, (local_idx >= 0) & (local_idx < rows_dev)

        def lookup_fast():
            cold = jnp.take(table_part, cold_idx, axis=0)
            hot = jnp.take(hot_rows.reshape(HOT_ROWS, width), hot_idx, axis=0)
            send = jnp.where((asked & is_hot)[:, None], hot, cold).reshape(N_DEV, CAP, width)
            got = lax.all_to_all(send, "fsdp", 0, 0, tiled=True)
            return jnp.take(got.reshape(N_DEV * CAP, width), token_place, axis=0)

        def lookup_dense():
            local_idx, is_owned = owned_index()
            looked = jnp.take(table_part, jnp.where(is_owned, local_idx, 0), axis=0)
            looked = jnp.where(is_owned[..., None], looked, jnp.zeros((), BF16))
            return lax.psum_scatter(looked, "fsdp", scatter_dimension=0)

        x_rows = lax.cond(fits, lookup_fast, lookup_dense)

        d_attn = lax.dot_general(grad_seq, wo_full, (((1,), (1,)), ((), ())), preferred_element_type=F32).astype(BF16)
        hidden, qkv = qkv_proj(x_rows, wqkv_full, gain_row, bias_row, cos_t, sin_t)
        attn_b, dq_b, dkv_b, dbq, dbkv = attention(qkv, d_attn, cos_t, sin_t, n_heads, kv_heads)
        d_x, dqkv_b, dgain = input_grad(dq_b, dkv_b, wqkv_full, x_rows, grad_seq, gain_row)

        rows_dims = (((0,), (0,)), ((), ()))
        grad_wo = lax.dot_general(attn_b, grad_seq, rows_dims, preferred_element_type=F32)
        grad_wqkv = lax.dot_general(hidden, dqkv_b, rows_dims, preferred_element_type=F32)
        proj_out = jnp.dot(attn_b, wo_full, preferred_element_type=F32)
        block_out = (x_rows.astype(F32) + proj_out).astype(BF16)
        grad_wo = lax.psum_scatter(grad_wo, "fsdp", scatter_dimension=0, tiled=True)
        grad_wqkv = lax.psum_scatter(grad_wqkv, "fsdp", scatter_dimension=0, tiled=True)

        def table_fast():
            packed = jnp.zeros((N_DEV * CAP, width), F32).at[token_place].add(d_x)
            got = lax.all_to_all(packed.reshape(N_DEV, CAP, width), "fsdp", 0, 0, tiled=True).reshape(N_DEV * CAP, width)
            dest = jnp.where(asked, jnp.where(is_hot, rows_dev + hot_idx, cold_idx), rows_dev + HOT_ROWS)
            summed = jnp.zeros((rows_dev + HOT_ROWS, width), F32).at[dest].add(got, mode="drop")
            hot_sums = summed[rows_dev:].astype(BF16).reshape(HOT_GROUPS, 8, width)
            returned = hot_return(hot_sums).reshape(HOT_IDS, width)
            low = jnp.where(me == 0, returned, summed[:HOT_IDS].astype(BF16))
            return jnp.concatenate([low, summed[HOT_IDS:rows_dev].astype(BF16)], axis=0)

        def table_dense():
            local_idx, is_owned = owned_index()
            all_dx = lax.all_gather(d_x, "fsdp")
            seg_idx = jnp.where(is_owned, local_idx, rows_dev)
            return jax.ops.segment_sum(all_dx.reshape(-1, width), seg_idx.reshape(-1), num_segments=rows_dev).astype(BF16)

        grad_table = lax.cond(fits, table_fast, table_dense)

        def kv_split(arr):
            ks = [arr[..., 2 * g * HEAD_DIM : (2 * g + 1) * HEAD_DIM] for g in range(kv_heads)]
            vs = [arr[..., (2 * g + 1) * HEAD_DIM : (2 * g + 2) * HEAD_DIM] for g in range(kv_heads)]
            return jnp.concatenate(ks, axis=-1), jnp.concatenate(vs, axis=-1)

        dbk, dbv = kv_split(dbkv.reshape(2 * kv_cols))
        vecs = jnp.concatenate(
            [dgain.reshape(N_DEV, n_g), dbq.reshape(N_DEV, n_q), dbk.reshape(N_DEV, n_kv), dbv.reshape(N_DEV, n_kv)], axis=1
        )
        vecs = lax.psum_scatter(vecs, "fsdp", scatter_dimension=0, tiled=True)[0]
        grad_wk, grad_wv = kv_split(grad_wqkv[:, q_cols:])
        return (
            block_out[None],
            grad_table,
            vecs[:n_g],
            grad_wqkv[:, :q_cols],
            vecs[n_g : n_g + n_q],
            grad_wk,
            vecs[n_g + n_q : n_g + n_q + n_kv],
            grad_wv,
            vecs[n_g + n_q + n_kv : n_small],
            grad_wo,
        )

    return jax.shard_map(device_step, mesh=mesh, in_specs=in_specs, out_specs=out_specs, check_vma=False)
```

time: 2170 us -> 1190 us (0.55)
  other arithmetic: 806 us -> 213 us
  Pallas kernels: 0 us -> 322 us
  matrix products: 363 us -> 55.1 us
  waiting for transfers between devices: 698 us -> 441 us
  local copies, waits for them, and re-layouts: 165 us -> 86.6 us
  blocking collectives: 107 us -> 30.8 us
    scatter-add x3 -> x4, other arithmetic: 528 us -> 111 us  [the longest x3 88.1 us: table_fast(): jnp.zeros((rows_dev + HOT_ROWS, width), F32).at[dest].add(got, mode='drop')]
    all_gather x2 -> x1, waiting for transfers between devices: 399 us -> 32.1 us  [device_step(): lax.all_gather(jnp.concatenate([wq_part] + kv_order(wk_part, wv_part), ax...]
    pallas_call x0 -> x5, Pallas kernels: none -> 322 us  [the longest x1 138 us: attention(): pl.pallas_call(attention_kernel, grid=grid, out_shape=(jax.ShapeDtypeStru...]
    dot_general x18 -> x4, matrix products: 363 us -> 55.1 us  [the longest x1 16.6 us: device_step(): lax.dot_general(hidden, dqkv_b, rows_dims, preferred_element_type=F32)]
    all_to_all x0 -> x2, waiting for transfers between devices: none -> 260 us  [the longest x1 170 us: table_fast(): lax.all_to_all(packed.reshape(N_DEV, CAP, width), 'fsdp', 0, 0, tiled=True)]
    reduce_scatter x5 -> x2, waiting for transfers between devices: 297 us -> 114 us  [the longest x1 79.7 us: device_step(): grad_wo = lax.psum_scatter(grad_wo, 'fsdp', scatter_dimension=0, tiled=True)]
    gather x1 -> x3, local copies, waits for them, and re-layouts: 159 us -> 50.9 us  [the longest x1 27.9 us: lookup_fast(): cold = jnp.take(table_part, cold_idx, axis=0)]
    another operation x1, other arithmetic: 89.1 us -> 30.2 us
  transfers between devices with their start and end apart: 8 -> 6, of which waited for: 3 -> 6; matrix products, arithmetic and copies ran while one was open for 42% -> 5% of each run, Pallas kernels for 0% -> 0%
where the time goes in v1:
time: 1190 us; the launch traced here: 1180 us
  waiting for transfers between devices  441 us (37%)
  Pallas kernels  322 us (27%)
  other arithmetic  213 us (18%)
  local copies, waits for them, and re-layouts  86.6 us (7%)
  matrix products  55.1 us (5%)
  blocking collectives  30.8 us (3%)
  between operations  17.7 us (1%)
    all_to_all x1, waiting for transfers between devices, table_fast(): lax.all_to_all(packed.reshape(N_DEV, CAP, width), 'fsdp', 0, 0, tiled=True)  170 us
    pallas_call x1, Pallas kernels, attention(): pl.pallas_call(attention_kernel, grid=grid, out_shape=(jax.ShapeDtypeStru...  138 us
    all_to_all x1, waiting for transfers between devices, lookup_fast(): got = lax.all_to_all(send, 'fsdp', 0, 0, tiled=True)  89.9 us
    scatter-add x3, other arithmetic, table_fast(): jnp.zeros((rows_dev + HOT_ROWS, width), F32).at[dest].add(got, mode='drop')  88.1 us
    reduce_scatter x1, waiting for transfers between devices, device_step(): grad_wo = lax.psum_scatter(grad_wo, 'fsdp', scatter_dimension=0, tiled=True)  79.7 us
    pallas_call x1, Pallas kernels, head_exchange(): pl.pallas_call(head_exchange_kernel, out_shape=(jax.ShapeDtypeStruct((HOT...  76.1 us
    pallas_call x1, Pallas kernels, hot_return(): pl.pallas_call(hot_return_kernel, out_shape=jax.ShapeDtypeStruct((groups,...  71 us
    all_gather x1, waiting for transfers between devices, device_step(): wo_full = lax.all_gather(wo_part, 'fsdp', axis=0, tiled=True)  34.2 us
  transfers between devices with their start and end apart: 6, of which 6 were waited for; matrix products, arithmetic and copies ran while one was open for 5% of the time, Pallas kernels for 0%

profile of v1, /device:TPU:0, one launch (start us, length us, event | category | flops | bytes accessed | tf_op | source)
XLA Modules:
  0.0 1182.5 jit_solution(9166459287554581203)
XLA Ops:
  8.0 0.8 fusion.34
  8.8 2.7 fusion.17
  11.6 10.5 slice.128
  22.1 2.5 convert_reduce_fusion
  25.9 2.0 select_reduce_fusion
  28.0 0.7 reshape.228.req_ref
  29.4 76.1 %head_exchange.1 = (bf16[32,8,1536]{2,1,0:T(8,128)(2,1)S(1)}, s32[16,1,144]{2,1,0:T(1,128)}, f32[16,1,256]{2,1,0:T(1,128)}) custom-call(bf16[32,16,8,1536]{3,2,1,0:T(8,128)(2,1)} %bitcast.72, s32[16,1,144]{2,1,0:T(1,128)} %reshape.228.req_ref, f32[1,256]{1,0:T(1,128)} %bitcast.85), custom_call_target="tpu_custom_call" | custom-call | tf_op jit(solution)/shard_map/head_exchange/pallas_call | solution.py:86
  105.5 0.8 add_reduce_fusion
  106.4 0.7 copy.32
  107.7 0.7 slice_reduce_fusion
  109.1 159.3 %conditional.2 = (bf16[1536,1536]{1,0:T(8,128)(2,1)}) conditional(s32[]{:T(128)} %convert_element_type.37, (s32[1,1536]{1,0:T(1,128)S(1)}, s32[]{:T(128)}, bf16[9496,1536]{1,0:T(8,128)(2,1)}) %tuple.75, (s32[1536]{0:T(1024)S(1)}, pred[2304]{0:T(1024)(128)(4,1)S(1)}, pred[2304]{0:T(1024)(128)(4,1)S(1)}, s32[2304]{0:T(1024)S(1)}, ...), branch_computations={%region_5.7_spmd, %region_7.8_spmd} | conditional | flops 75964416 | bytes 544020608 | solution.py:408
  109.9 8.7 gather_fusion
  118.6 27.9 %gather_fusion.1 = bf16[2304,1536]{1,0:T(8,128)(2,1)} fusion(bf16[9496,1536]{1,0:T(8,128)(2,1)} %get-tuple-element.59, s32[3072]{0:T(1024)S(1)} %pad_clamp_fusion), kind=kCustom, calls=%fused_computation.2 | custom fusion | bytes 14164992 | tf_op jit(solution)/shard_map/cond/branch_1_fun/jit(_take)/gather | solution.py:396
  146.5 8.6 select_select_fusion.1
  155.1 3.9 all-to-all-start
  159.0 89.9 %all-to-all-done = bf16[16,144,1536]{2,1,0:T(8,128)(2,1)} async-done(((bf16[16,144,1536]{2,1,0:T(8,128)(2,1)}), bf16[16,144,1536]{2,1,0:T(8,128)(2,1)}, u32[]{:S(2)}, u32[]{:S(2)}) %all-to-all-start) | async-done | bytes 7077920 | tf_op jit(solution)/shard_map/cond/branch_1_fun/all_to_all | solution.py:399
  248.9 14.3 %gather_fusion.2 = bf16[1536,1536]{1,0:T(8,128)(2,1)} fusion(bf16[2304,1536]{1,0:T(8,128)(2,1)} %bitcast.6, s32[2048]{0:T(1024)S(1)} %pad_clamp_fusion.2), kind=kCustom, calls=%fused_computation.3 | custom fusion | bytes 9443328 | tf_op jit(solution)/shard_map/cond/branch_1_fun/jit(_take)/gather | solution.py:400
  263.2 5.0 broadcast_select_fusion
  269.2 0.7 copy-done
  270.5 0.7 reshape.229.gain_ref
  271.3 2.9 fusion.21
  274.2 1.7 pad_maximum_fusion.1
  275.9 34.2 %all-gather.11.cloned.1.call-done = bf16[1536,1536]{1,0:T(8,128)(2,1)} async-done(((bf16[96,1536]{1,0:T(8,128)(2,1)}), bf16[1536,1536]{1,0:T(8,128)(2,1)}) %all-gather.11.cloned.1.call-update) | async-done | bytes 4718608 | tf_op jit(solution)/shard_map/all_gather | solution.py:366
  310.1 12.4 %convolution_convert_fusion.do_ref = bf16[1536,1536]{1,0:T(8,128)(2,1)} fusion(bf16[1536,1536]{1,0:T(8,128)(2,1)} %all-gather.11.cloned.1.call-done, bf16[1,1536,1536]{2,1,0:T(8,128)(2,1)} %param.16), kind=kOutput, calls=%fused_computation.56 | convolution fusion | flops 7250116608 | bytes 14155776 | tf_op jit(solution)/shard_map/dot_general | solution.py:410
  322.4 32.1 %all-gather.9.cloned.1.call-done.w_ref = bf16[1536,2048]{1,0:T(8,128)(2,1)} async-done(((bf16[96,2048]{1,0:T(8,128)(2,1)}), bf16[1536,2048]{1,0:T(8,128)(2,1)}) %all-gather.9.cloned.1.call-update) | async-done | bytes 6291472 | tf_op jit(solution)/shard_map/all_gather | solution.py:365
  354.5 16.7 %qkv_proj.1 = (bf16[1536,1536]{1,0:T(8,128)(2,1)}, bf16[1536,2048]{1,0:T(8,128)(2,1)}) custom-call(bf16[1536,1536]{1,0:T(8,128)(2,1)} %get-tuple-element.150.x_ref, bf16[1536,2048]{1,0:T(8,128)(2,1)} %all-gather.9.cloned.1.call-done.w_ref, f32[1,1536]{1,0:T(1,128)} %reshape.229.gain_ref, f32[1,2048]{1,0:T(1,128)} %bitcast.88, ...), custom_call_target="tpu_custom_call" | custom-call | flops 9663676416 | bytes 20000000 | tf_op jit(solution)/shard_map/qkv_proj/pallas_call | solution.py:165
  371.2 138.3 %attention.1 = (bf16[1536,1536]{1,0:T(8,128)(2,1)}, bf16[1536,1536]{1,0:T(8,128)(2,1)}, bf16[1536,512]{1,0:T(8,128)(2,1)}, f32[12,1,128]{2,1,0:T(1,128)}, f32[2,1,256]{2,1,0:T(1,128)}) custom-call(bf16[1536,2048]{1,0:T(8,128)(2,1)} %get-tuple-element.96.q_ref.k_ref.v_ref, bf16[1536,2048]{1,0:T(8,128)(2,1)} %get-tuple-element.96.q_ref.k_ref.v_ref, ...), custom_call_target="tpu_custom_call" | custom-call | flops 43486543872 | bytes 25000000 | tf_op jit(solution)/shard_map/attention/pallas_call | solution.py:242
  509.6 19.6 %input_grad.1 = (f32[1536,1536]{1,0:T(8,128)}, bf16[1536,2048]{1,0:T(8,128)(2,1)}, f32[1,1536]{1,0:T(1,128)}) custom-call(bf16[1536,1536]{1,0:T(8,128)(2,1)} %get-tuple-element.98.dq_ref, bf16[1536,512]{1,0:T(8,128)(2,1)} %get-tuple-element.99.dkv_ref, bf16[1536,2048]{1,0:T(8,128)(2,1)} %all-gather.9.cloned.1.call-done.w_ref, ...), custom_call_target="tpu_custom_call" | custom-call | flops 9663676416 | bytes 40000000 | tf_op jit(solution)/shard_map/input_grad/pallas_call | solution.py:305
  529.2 16.6 %fusion.42 = f32[1536,2048]{1,0:T(8,128)} fusion(bf16[1536,1536]{1,0:T(8,128)(2,1)} %get-tuple-element.104, bf16[1536,2048]{1,0:T(8,128)(2,1)} %get-tuple-element.105), kind=kOutput, calls=%fused_computation.139 | convolution fusion | flops 9663676416 | bytes 23592960 | tf_op jit(solution)/shard_map/dot_general | solution.py:417
  545.8 451.2 %conditional.3 = (bf16[9496,1536]{1,0:T(8,128)(2,1)}) conditional(s32[]{:T(128)} %convert_element_type.37, (s32[1,1536]{1,0:T(1,128)S(1)}, s32[]{:T(128)}, f32[1536,1536]{1,0:T(8,128)}) %tuple.76, (s32[]{:T(128)}, s32[2304]{0:T(1024)S(1)}, pred[2304]{0:T(1024)(128)(4,1)S(1)}, s32[2304]{0:T(1024)S(1)}, pred[2304]{0:T(1024)(128)(4,1)S(1)}, ...), branch_computations={%region_8.10_spmd, %region_10.13_spmd} | conditional | flops 85561344 | bytes 628537920 | solution.py:439
  554.3 22.7 %scatter_custom_fusion.1 = f32[2304,1536]{1,0:T(8,128)} fusion(s32[1536]{0:T(1024)S(1)} %compare_select_fusion.5, f32[1536,1536]{1,0:T(8,128)} %get-tuple-element.69, f32[]{:T(128)} %constant.161.clone), kind=kCustom, calls=%fused_computation.43 | custom fusion | flops 2359296 | bytes 14156288 | tf_op jit(solution)/shard_map/cond/branch_1_fun/scatter-add | solution.py:424
  577.0 3.8 all-to-all-start.1
  580.8 5.2 sort.1
  586.0 169.8 %all-to-all-done.1 = f32[16,144,1536]{2,1,0:T(8,128)} async-done(((f32[16,144,1536]{2,1,0:T(8,128)}), f32[16,144,1536]{2,1,0:T(8,128)}, u32[]{:S(2)}, u32[]{:S(2)}) %all-to-all-start.1) | async-done | bytes 14155808 | tf_op jit(solution)/shard_map/cond/branch_1_fun/all_to_all | solution.py:425
  755.8 82.9 %scatter_custom_fusion.2 = f32[9752,1536]{1,0:T(8,128)} fusion(s32[2304]{0:T(1024)S(1)} %get-tuple-element.108, f32[]{:T(128)} %constant.161.clone, f32[2304,1536]{1,0:T(8,128)} %bitcast.9, s32[3072]{0:T(1024)S(1)} %pad_clamp_fusion.3), kind=kCustom, calls=%fused_computation.38 | custom fusion | flops 3538944 | bytes 59916800 | tf_op jit(solution)/shard_map/cond/branch_1_fun/scatter-add | solution.py:427
  838.7 30.2 %convert.4 = bf16[9752,1536]{1,0:T(8,128)(2,1)} convert(f32[9752,1536]{1,0:T(8,128)} %scatter_custom_fusion.2) | non-fusion elementwise | flops 14979072 | bytes 89874432 | tf_op jit(solution)/shard_map/convert.2
  869.0 2.1 slice_bitcast_fusion.sums_ref
  871.0 13.8 %slice.176 = bf16[5400,1536]{1,0:T(8,128)(2,1)} slice(bf16[9752,1536]{1,0:T(8,128)(2,1)} %convert.4), slice={[4096:9496], [0:1536]} | slice | bytes 33177600 | tf_op jit(solution)/shard_map/cond/branch_1_fun/slice | solution.py:431
  884.8 71.0 %hot_return.1 = bf16[32,16,8,1536]{3,2,1,0:T(8,128)(2,1)} custom-call(bf16[32,8,1536]{2,1,0:T(8,128)(2,1)} %slice_bitcast_fusion.sums_ref), custom_call_target="tpu_custom_call" | custom-call | tf_op jit(solution)/shard_map/cond/branch_1_fun/hot_return/pallas_call | solution.py:128
  955.8 13.3 %slice_select_fusion = bf16[4096,1536]{1,0:T(8,128)(2,1)} fusion(bf16[9752,1536]{1,0:T(8,128)(2,1)} %convert.4, bf16[32,16,8,1536]{3,2,1,0:T(8,128)(2,1)} %hot_return.1, pred[]{:T(512)S(6)} %eq.3), kind=kLoop, calls=%fused_computation.42 | loop fusion | flops 6291456 | bytes 37748736 | tf_op jit(solution)/shard_map/cond/branch_1_fun/jit(_where)/select_n | solution.py:430
  969.1 27.6 %pad_maximum_fusion = bf16[9496,1536]{1,0:T(8,128)(2,1)} fusion(bf16[5400,1536]{1,0:T(8,128)(2,1)} %slice.176, bf16[4096,1536]{1,0:T(8,128)(2,1)} %slice_select_fusion), kind=kLoop, calls=%fused_computation.40 | loop fusion | flops 58343424 | bytes 58343424 | tf_op jit(solution)/shard_map/cond/branch_1_fun/concatenate | solution.py:431
  997.6 13.2 %fusion.35 = f32[1536,1536]{1,0:T(8,128)} fusion(bf16[1536,1536]{1,0:T(8,128)(2,1)} %get-tuple-element.97, bf16[1,1536,1536]{2,1,0:T(8,128)(2,1)} %param.16), kind=kOutput, calls=%fused_computation.132 | convolution fusion | flops 7247757312 | bytes 18874368 | tf_op jit(solution)/shard_map/dot_general | solution.py:416
  1011.9 30.8 %all-reduce = f32[16,224]{1,0:T(8,128)S(1)} all-reduce(f32[16,224]{1,0:T(8,128)S(1)} %maximum_maximum_fusion), channel_id=4, replica_groups=mesh['fsdp'=16] {'fsdp'}, use_global_device_ids=true, to_apply=%region_13.14.clone | all-reduce | flops 3584 | bytes 28672
  1043.8 12.9 %fusion.18 = bf16[1,1536,1536]{2,1,0:T(8,128)(2,1)} fusion(bf16[1536,1536]{1,0:T(8,128)(2,1)} %get-tuple-element.97, bf16[1536,1536]{1,0:T(8,128)(2,1)} %all-gather.11.cloned.1.call-done, bf16[1536,1536]{1,0:T(8,128)(2,1)} %get-tuple-element.150.x_ref), kind=kOutput, calls=%fused_computation.57 | convolution fusion | flops 7254835200 | bytes 18874368 | tf_op jit(solution)/shard_map/dot_general | solution.py:418
  1056.7 34.0 %reduce-scatter.6.cloned.1.call-done = f32[96,2048]{1,0:T(8,128)} async-done(((f32[1536,2048]{1,0:T(8,128)}), f32[96,2048]{1,0:T(8,128)}) %reduce-scatter.6.cloned.1.call-update) | async-done | bytes 786448 | tf_op jit(solution)/shard_map/reduce_scatter | solution.py:421
  1090.7 1.9 slice.188
  1092.6 0.9 fusion.38
  1094.8 79.7 %reduce-scatter.8.cloned.1.call-done = f32[96,1536]{1,0:T(8,128)} async-done(((f32[1536,1536]{1,0:T(8,128)}), f32[96,1536]{1,0:T(8,128)}) %reduce-scatter.8.cloned.1.call-update) | async-done | bytes 589840 | tf_op jit(solution)/shard_map/reduce_scatter | solution.py:420
  (92 shorter events, 7.9 us)
Async XLA Ops:
  11.6 17.1 %copy-start.12 = (bf16[16]{0:T(256)(128)(2,1)S(1)}, bf16[16]{0:T(256)(128)(2,1)}, u32[]{:S(2)}) copy-start(bf16[16]{0:T(256)(128)(2,1)} %param.24) | copy-start | bytes 100
  11.6 17.1 %copy-start.13 = (bf16[16]{0:T(256)(128)(2,1)S(1)}, bf16[16]{0:T(256)(128)(2,1)}, u32[]{:S(2)}) copy-start(bf16[16]{0:T(256)(128)(2,1)} %param.22) | copy-start | bytes 100
  11.6 17.1 %copy-start.14 = (bf16[96]{0:T(256)(128)(2,1)S(1)}, bf16[96]{0:T(256)(128)(2,1)}, u32[]{:S(2)}) copy-start(bf16[96]{0:T(256)(128)(2,1)} %param.20) | copy-start | bytes 580
  11.6 17.1 %copy-start.15 = (bf16[96]{0:T(256)(128)(2,1)S(1)}, bf16[96]{0:T(256)(128)(2,1)}, u32[]{:S(2)}) copy-start(bf16[96]{0:T(256)(128)(2,1)} %param.18) | copy-start | bytes 580
  22.1 86.9 %copy-start.6 = (s32[1,1536]{1,0:T(1,128)S(1)}, s32[1,1536]{1,0:T(1,128)}, u32[]{:S(2)}) copy-start(s32[1,1536]{1,0:T(1,128)} %param.15) | copy-start | bytes 18436
  107.1 0.6 copy-start.2
  109.0 160.0 %copy-start.1 = (bf16[96,1536]{1,0:T(8,128)(2,1)S(1)}, bf16[96,1536]{1,0:T(8,128)(2,1)}, u32[]{:S(2)}) copy-start(bf16[96,1536]{1,0:T(8,128)(2,1)} %param.19) | copy-start | bytes 884740
  109.1 160.0 %copy-start.7 = (bf16[96,256]{1,0:T(8,128)(2,1)S(1)}, bf16[96,256]{1,0:T(8,128)(2,1)}, u32[]{:S(2)}) copy-start(bf16[96,256]{1,0:T(8,128)(2,1)} %param.21) | copy-start | bytes 147460
  109.1 160.0 %copy-start.8 = (bf16[96,256]{1,0:T(8,128)(2,1)S(1)}, bf16[96,256]{1,0:T(8,128)(2,1)}, u32[]{:S(2)}) copy-start(bf16[96,256]{1,0:T(8,128)(2,1)} %param.23) | copy-start | bytes 147460
  109.1 160.9 %copy-start.3 = (f32[16,1,256]{2,0,1:T(8,128)S(1)}, f32[16,1,256]{2,0,1:T(8,128)}, u32[]{:S(2)}) copy-start(f32[16,1,256]{2,0,1:T(8,128)} %copy-done.2) | copy-start | bytes 49156
  155.1 93.8 %all-to-all-start = ((bf16[16,144,1536]{2,1,0:T(8,128)(2,1)}), bf16[16,144,1536]{2,1,0:T(8,128)(2,1)}, u32[]{:S(2)}, u32[]{:S(2)}) async-start(bf16[16,144,1536]{2,1,0:T(8,128)(2,1)} %select_select_fusion.1), calls=%async_computation.1 | async-start | bytes 14155776 | tf_op jit(solution)/shard_map/cond/branch_1_fun/all_to_all | solution.py:399
  268.4 41.7 %all-gather.11.cloned.1.call-start = ((), (), s32[]{:S(2)}) async-start(), calls=%async_computation.8 | async-start | bytes 5013504 | tf_op jit(solution)/shard_map/all_gather | solution.py:366
  269.0 85.5 %all-gather.9.cloned.1.call-start = ((), (), s32[]{:S(2)}) async-start(), calls=%async_computation.7 | async-start | bytes 6684672 | tf_op jit(solution)/shard_map/all_gather | solution.py:365
  269.2 0.7 copy-start
  271.2 51.2 %copy-start.16 = (f32[2048]{0:T(1024)}, f32[2048]{0:T(1024)S(1)}, u32[]{:S(2)}) copy-start(f32[2048]{0:T(1024)S(1)} %constant_dynamic-update-slice_fusion.2) | copy-start | bytes 24580
  577.0 178.8 %all-to-all-start.1 = ((f32[16,144,1536]{2,1,0:T(8,128)}), f32[16,144,1536]{2,1,0:T(8,128)}, u32[]{:S(2)}, u32[]{:S(2)}) async-start(f32[16,144,1536]{2,1,0:T(8,128)} %bitcast.71), calls=%async_computation.2 | async-start | bytes 28311552 | tf_op jit(solution)/shard_map/cond/branch_1_fun/all_to_all | solution.py:425
  997.0 93.7 %reduce-scatter.6.cloned.1.call-start = ((), (), s32[]{:S(2)}) async-start(), calls=%async_computation.9 | async-start | bytes 13369344 | tf_op jit(solution)/shard_map/reduce_scatter | solution.py:421
  997.6 176.9 %reduce-scatter.8.cloned.1.call-start = ((), (), s32[]{:S(2)}) async-start(), calls=%async_computation.10 | async-start | bytes 10027008 | tf_op jit(solution)/shard_map/reduce_scatter | solution.py:420
  1010.8 0.7 copy-start.10
  1010.8 0.8 copy-start.11
  1010.8 0.8 copy-start.9
Sparse Core Ops, SparseCore 1:
  271.1 38.9 all-gather.10
  312.8 41.7 all-gather.8
  1002.1 88.6 reduce-scatter.5
  1096.0 78.4 reduce-scatter.7
